TPU v7x, 32 devices: a whole 2x2x4 slice. The times are simulated.
32 devices in a mesh: grp: 4 (over y, x), mem: 8 (over z, core).
Axes of the slice: x: 2, y: 2, z: 4, core: 2. Of those that a mesh axis runs over, the one named last changes fastest.
Arguments:
- params: float32 [4, 2048, 2048], P('grp', 'mem'), may hold values from -6 to 6
- estimate: float32 [4, 2048, 2048], P('grp', 'mem'), may hold values from -6 to 6
- mixed_sum: float32 [4, 2048, 2048], P('grp', 'mem'), may hold values from -6 to 6
- activations: bfloat16 [32768, 2048], P(('grp', 'mem')), may hold values from -6 to 6
- out_grads: bfloat16 [32768, 2048], P(('grp', 'mem')), may hold values from -6 to 6
- exponents: int32 [4, 32], P('grp', 'mem'), may hold values from 0 to 3
- edge_weight: float32 [4], replicated, may hold values from 0.1 to 0.45
Outputs:
- new_params: float32 [4, 2048, 2048], P('grp', 'mem')
- new_estimate: float32 [4, 2048, 2048], P('grp', 'mem')
- new_mixed: float32 [4, 2048, 2048], P('grp', 'mem')
All inputs are finite; a program needn't handle non-finite values.
Results may differ from a plain program's by a relative error of at most 0.01.
Values may be sent and summed in bfloat16 or wider, within the bound.
A program may use at most 128 MiB of HBM per device.

v0:
```python
import functools
import math

import jax
import jax.numpy as jnp
from jax import lax
from jax.experimental import pallas as pl
from jax.experimental.pallas import tpu as pltpu
from jax.sharding import PartitionSpec as P

step_size = 0.5
mixing_rate = 0.4
CHUNKS = 8
DEPTH = 3
LAG = 2
MESH = pl.DeviceIdType.MESH
f32 = jnp.float32
bf16 = jnp.bfloat16


def kernel(
    cfg,
    params, estimate, mixed, acts, grads, exponents, edges,
    out_params, out_estimate, out_mixed,
    act_v, act_t, grad_v, par_v, est_v, mix_v,
    mine, give, got, line_out, line_in, own, near, far,
    act_sem, grad_sem, par_sem, est_sem, mix_sem,
    pair_s, pair_r, line_s, line_r, near_s, near_r, far_s, far_r,
):
    members, groups, chunks, rows, width, tokens, factor = cfg
    chips = members // 2
    pairs = chips // 2
    items = pairs * chunks
    slots = (chips - 1) * chunks
    cols = width // chunks
    g = lax.axis_index("grp")
    m = lax.axis_index("mem")
    chip, core = m // 2, m % 2
    other = 1 - core
    sibling = chip * 2 + other
    line_to = [
        lax.rem(chip + 1, chips) * 2 + core,
        lax.rem(chip + chips - 1, chips) * 2 + core,
    ]
    place = [chip, chips - 1 - chip]
    odd = g % 2
    partner = g + 1 - 2 * odd
    onward = lax.rem(g + 2 - 4 * odd + groups, groups)
    backward = lax.rem(g + groups - 2 + 4 * odd, groups)

    def act_copy(block):
        return pltpu.make_async_copy(
            acts.at[:, pl.ds(pl.multiple_of(block * rows, rows), rows)],
            act_v.at[block],
            act_sem.at[block],
        )

    def chunk_of(ref, j):
        return ref.at[:, pl.ds(pl.multiple_of(j * cols, cols), cols)]

    def grad_copy(j):
        return pltpu.make_async_copy(chunk_of(grads, j), grad_v.at[j], grad_sem.at[j])

    def load_copies(j):
        return [
            pltpu.make_async_copy(chunk_of(src.at[0], j), dst.at[j], sem.at[j])
            for src, dst, sem in (
                (params, par_v, par_sem), (estimate, est_v, est_sem), (mixed, mix_v, mix_sem)
            )
        ]

    def lanes(j):
        return pl.ds(pl.multiple_of(j * cols, cols), cols)

    def pair_copy(i):
        return pltpu.make_async_remote_copy(
            src_ref=give.at[i], dst_ref=got.at[i],
            send_sem=pair_s.at[i], recv_sem=pair_r.at[i],
            device_id={"mem": sibling}, device_id_type=MESH,
        )

    def line_copy(way, slot):
        return pltpu.make_async_remote_copy(
            src_ref=line_out.at[way, slot], dst_ref=line_in.at[way, slot],
            send_sem=line_s.at[way, slot], recv_sem=line_r.at[way, slot],
            device_id={"mem": line_to[way]}, device_id_type=MESH,
        )

    def near_copy(j):
        return pltpu.make_async_remote_copy(
            src_ref=own.at[j], dst_ref=near.at[j],
            send_sem=near_s.at[j], recv_sem=near_r.at[j],
            device_id={"grp": partner}, device_id_type=MESH,
        )

    def far_copy(j):
        return pltpu.make_async_remote_copy(
            src_ref=near.at[j], dst_ref=far.at[j],
            send_sem=far_s.at[j], recv_sem=far_r.at[j],
            device_id={"grp": onward}, device_id_type=MESH,
        )

    def members_of(b):
        return [(b, other), (chips - 1 - b, other), (b, core), (chips - 1 - b, core)]

    barrier = pltpu.get_barrier_semaphore()
    for peer in (
        {"mem": sibling}, {"mem": line_to[0]}, {"mem": line_to[1]},
        {"grp": partner}, {"grp": onward}, {"grp": backward},
    ):
        pl.semaphore_signal(barrier, inc=1, device_id=peer, device_id_type=MESH)

    grad_copy(0).start()
    for b in range(pairs):
        for dest, parity in members_of(b):
            act_copy(dest * 2 + parity).start()
        if b == 0:
            for j in range(1, chunks):
                grad_copy(j).start()
    for j in range(chunks):
        for copy in load_copies(j):
            copy.start()

    def multiply(i, before_send):
        b, j = i // chunks, i % chunks

        @pl.when(b == 0)
        def _():
            grad_copy(j).wait()

        def turn(dest, parity):
            @pl.when(j == 0)
            def _():
                block = dest * 2 + parity
                act_copy(block).wait()
                act_t[block] = act_v[block].T

        def product(dest, parity):
            return jnp.dot(
                act_t[dest * 2 + parity], grad_v[j], preferred_element_type=f32
            ).astype(bf16)

        for which, dest in ((0, b), (1, chips - 1 - b)):
            turn(dest, other)
            give[i, which] = product(dest, other)
        before_send()
        pair_copy(i).start()
        for which, dest in ((0, b), (1, chips - 1 - b)):
            turn(dest, core)
            mine[i, which] = product(dest, core)

    def pair_sum(i, which):
        return mine[i, which].astype(f32) + got[i, which].astype(f32)

    def pass_on(way, t):
        slot = t - LAG * place[way]
        block = slot // chunks
        j = slot % chunks

        @pl.when(jnp.logical_and(slot >= 0, slot < (chips - 1 - place[way]) * chunks))
        def _():
            @pl.when(slot >= DEPTH)
            def _():
                line_copy(way, slot - DEPTH).wait_send()

            late = block >= pairs
            i = jnp.where(late, chips - 1 - block, block) * chunks + j
            which = jnp.where(late, way, 1 - way)

            @pl.when(place[way] == 0)
            def _():
                line_out[way, slot] = pair_sum(i, which).astype(bf16)

            @pl.when(place[way] > 0)
            def _():
                line_copy(way, slot).wait_recv()
                line_out[way, slot] = (
                    pair_sum(i, which) + line_in[way, slot].astype(f32)
                ).astype(bf16)

            line_copy(way, slot).start()

    weight_right = edges[g]
    weight_left = edges[lax.rem(g + groups - 1, groups)]
    weight_self = 1.0 - weight_left - weight_right
    weight_near = jnp.where(odd == 1, weight_left, weight_right)
    weight_far = jnp.where(odd == 1, weight_right, weight_left)
    blocks = exponents.shape[1]
    block_rows = rows // blocks
    first = jnp.int32(0)
    for c in range(chips):
        after = [(chips - 1 - c) * chunks + LAG * c] if c > 0 else []
        if c < chips - 1:
            after.append(c * chunks + LAG * (chips - 1 - c))
        first = jnp.where(chip == c, max(after), first)
    own_which = jnp.where(chip >= pairs, 1, 0)
    own_block = jnp.where(chip >= pairs, chips - 1 - chip, chip)

    def compress(j):
        slot_of = [(chips - 1 - place[way]) * chunks + j for way in (0, 1)]
        for way in (0, 1):
            @pl.when(place[way] > 0)
            def _(way=way):
                line_copy(way, slot_of[way]).wait_recv()

            @pl.when(place[way] == 0)
            def _(way=way):
                line_in[way, slot_of[way]] = jnp.zeros((rows, cols), bf16)

        for copy in load_copies(j):
            copy.wait()
        i = own_block * chunks + j
        for b in range(blocks):
            exponent = exponents[0, b]
            scale = (jnp.int32(1) << exponent).astype(f32)
            inverse = (jnp.int32(1) << (15 - exponent)).astype(f32) * (2.0 ** -15)
            at = pl.ds(b * block_rows, block_rows)
            gradient = (
                mine[i, own_which, at, :].astype(f32)
                + got[i, own_which, at, :].astype(f32)
                + line_in[0, slot_of[0], at, :].astype(f32)
                + line_in[1, slot_of[1], at, :].astype(f32)
            )
            stepped = par_v[j, at, :] - factor * gradient
            base = est_v[j, at, :]
            levels = jnp.clip((stepped - base) * inverse, -1.0, 1.0).astype(bf16)
            compressed = levels.astype(f32) * scale
            own[j, at, :] = compressed.astype(bf16)
            out_params[0, at, lanes(j)] = stepped
            out_estimate[0, at, lanes(j)] = base + compressed
            out_mixed[0, at, lanes(j)] = mix_v[j, at, :] + weight_self * compressed
        near_copy(j).start()

    def forward(j):
        near_copy(j).wait_recv()
        far_copy(j).start()

    def finish(j):
        far_copy(j).wait_recv()
        total = (
            out_mixed[0, :, lanes(j)] + weight_near * near[j].astype(f32) + weight_far * far[j].astype(f32)
        )
        out_mixed[0, :, lanes(j)] = total
        out_params[0, :, lanes(j)] = out_params[0, :, lanes(j)] + mixing_rate * (
            total - out_estimate[0, :, lanes(j)]
        )

    def guarded(run, j, count):
        @pl.when(jnp.logical_and(j >= 0, j < count))
        def _():
            run(j)

    multiply(0, lambda: pl.semaphore_wait(barrier, 6))
    multiply(1, lambda: None)

    def body(t, carry):
        guarded(lambda i: pair_copy(i).wait_recv(), t, items)
        for way in (0, 1):
            pass_on(way, t)
        guarded(compress, t - first, chunks)
        guarded(forward, t - first - LAG, chunks)
        guarded(finish, t - first - 2 * LAG, chunks)
        guarded(lambda i: multiply(i, lambda: None), t + 2, items)
        return carry

    lax.fori_loop(0, slots + LAG * (chips + 1), body, 0)

    def drain_pair(i, carry):
        pair_copy(i).wait_send()
        return carry

    def drain_line(slot, carry):
        for way in (0, 1):
            count = (chips - 1 - place[way]) * chunks

            @pl.when(jnp.logical_and(slot < count, slot >= count - DEPTH))
            def _(way=way):
                line_copy(way, slot).wait_send()
        return carry

    def drain(j, carry):
        near_copy(j).wait_send()
        far_copy(j).wait_send()
        return carry

    lax.fori_loop(0, items, drain_pair, 0)
    lax.fori_loop(0, slots, drain_line, 0)
    lax.fori_loop(0, chunks, drain, 0)


def on_device(members, groups, params, estimate, mixed, acts, grads, exponents, edges):
    rows, width = params.shape[1:]
    tokens = acts.shape[0]
    chunks = CHUNKS
    cols = width // chunks
    chips = members // 2
    items = chips // 2 * chunks
    slots = (chips - 1) * chunks
    factor = step_size / math.sqrt(members * tokens)
    cfg = (members, groups, chunks, rows, width, tokens, factor)
    wide = (chunks, rows, cols)
    tall = (items, 2, rows, cols)
    dma = pltpu.SemaphoreType.DMA
    any_spec = pl.BlockSpec(memory_space=pl.ANY)
    smem = pl.BlockSpec(memory_space=pltpu.SMEM)
    return pl.pallas_call(
        functools.partial(kernel, cfg),
        out_shape=[pltpu.VMEM(params.shape, f32)] * 3,
        in_specs=[any_spec] * 5 + [smem] * 2,
        out_specs=[pl.BlockSpec(memory_space=pltpu.VMEM)] * 3,
        scratch_shapes=[
            pltpu.VMEM((members, tokens, rows), bf16),
            pltpu.VMEM((members, rows, tokens), bf16),
            pltpu.VMEM((chunks, tokens, cols), bf16),
            *[pltpu.VMEM(wide, f32)] * 3,
            *[pltpu.VMEM(tall, bf16)] * 3,
            pltpu.VMEM((2, slots, rows, cols), bf16),
            pltpu.VMEM((2, slots + chunks, rows, cols), bf16),
            *[pltpu.VMEM(wide, bf16)] * 3,
            dma((members,)), dma((chunks,)), dma((chunks,)), dma((chunks,)), dma((chunks,)),
            dma((items,)), dma((items,)), dma((2, slots)), dma((2, slots)),
            dma((chunks,)), dma((chunks,)), dma((chunks,)), dma((chunks,)),
        ],
        compiler_params=pltpu.CompilerParams(
            collective_id=0, has_side_effects=True, vmem_limit_bytes=53 * 1024 * 1024
        ),
    )(params, estimate, mixed, acts, grads, exponents, edges)


def solution(mesh):
    shard = P("grp", "mem", None)
    tokens = P(("grp", "mem"), None)
    return jax.shard_map(
        functools.partial(on_device, mesh.shape["mem"], mesh.shape["grp"]),
        mesh=mesh,
        in_specs=(shard, shard, shard, tokens, tokens, P("grp", "mem"), P()),
        out_specs=(shard, shard, shard),
        check_vma=False,
    )
```

profile of v0, /device:TPU:16, one launch (start us, length us, event | category | flops | bytes accessed | tf_op | source)
XLA Modules:
  0.0 92.8 jit_solution(16656973109615071791)
XLA Ops:
  0.6 88.2 %shard_map.94 = (f32[1,256,2048]{2,1,0:T(8,128)S(1)}, f32[1,256,2048]{2,1,0:T(8,128)S(1)}, f32[1,256,2048]{2,1,0:T(8,128)S(1)}) custom-call(f32[1,256,2048]{2,1,0:T(8,128)} %params.1, f32[1,256,2048]{2,1,0:T(8,128)} %estimate.1, f32[1,256,2048]{2,1,0:T(8,128)} %mixed.1, bf16[1024,2048]{1,0:T(8,128)(2,1)} %acts.1, bf16[1024,2048]{1,0:T(8,128)(2,1)} %grads.1, ...), custom_call_target="tpu_custom_call" | custom-call | tf_op jit(solution)/shard_map/pallas_call | solution.py:306
  88.9 1.3 %copy.13 = f32[1,256,2048]{2,1,0:T(8,128)} copy(f32[1,256,2048]{2,1,0:T(8,128)S(1)} %get-tuple-element.3) | data formatting | bytes 4194304
  90.2 1.3 %copy.14 = f32[1,256,2048]{2,1,0:T(8,128)} copy(f32[1,256,2048]{2,1,0:T(8,128)S(1)} %get-tuple-element.4) | data formatting | bytes 4194304
  91.5 1.3 %copy.15 = f32[1,256,2048]{2,1,0:T(8,128)} copy(f32[1,256,2048]{2,1,0:T(8,128)S(1)} %get-tuple-element.5) | data formatting | bytes 4194304
where the time goes:
time: 93.1 us; the launch traced here: 92.8 us
  Pallas kernels  88.2 us (95%)
  local copies, waits for them, and re-layouts  3.96 us (4%)
    pallas_call x1, Pallas kernels, on_device(): pl.pallas_call(functools.partial(kernel, cfg), out_shape=[pltpu.VMEM(para...  88.2 us
    unnamed x3, local copies, waits for them, and re-layouts  3.96 us

commit v1 on v0

v1 whole, which is shorter than its diff:
```python
import functools
import math

import jax
import jax.numpy as jnp
from jax import lax
from jax.experimental import pallas as pl
from jax.experimental.pallas import tpu as pltpu
from jax.sharding import PartitionSpec as P

step_size = 0.5
mixing_rate = 0.4
CHUNKS = 16
DEPTH = 3
LAG = 2
RELAY = 2
GOSSIP = 4
DIRECT = 1
PIECES = 4
SPLIT = 2
SLOTS = 4
RING = 8
MESH = pl.DeviceIdType.MESH
f32 = jnp.float32
bf16 = jnp.bfloat16


def kernel(
    cfg,
    params, estimate, mixed, acts, grads, exponents, edges,
    out_params, out_estimate, out_mixed,
    act_v, act_t, grad_v, par_v, est_v, mix_v,
    mine, give, got, line_out, line_in, own, near, far,
    act_sem, grad_sem, load_sem,
    pair_s, half_r, pair_r, line_s, line_r, near_s, near_r, far_s, far_r,
):
    members, groups, chunks, rows, width, tokens, factor = cfg
    chips = members // 2
    pairs = chips // 2
    steps = chips - 1
    cols = width // chunks
    g = lax.axis_index("grp")
    m = lax.axis_index("mem")
    chip, core = m // 2, m % 2
    other = 1 - core
    sibling = chip * 2 + other
    line_to = [
        lax.rem(chip + 1, chips) * 2 + core,
        lax.rem(chip + chips - 1, chips) * 2 + core,
    ]
    place = [chip, chips - 1 - chip]
    odd = g % 2
    near_to = lax.rem(g + groups + 1 - 2 * odd, groups)
    far_to = lax.rem(g + groups - 1 + 2 * odd, groups)
    onward = lax.rem(g + groups + 2 - 4 * odd, groups)
    backward = lax.rem(g + groups - 2 + 4 * odd, groups)

    begin = [2 * s + 3 if s else 0 for s in range(pairs)]
    for s in range(pairs, steps):
        begin.append(begin[-1] + 1)
    first = jnp.int32(0)
    last = 0
    for c in range(chips):
        after = max(begin[steps - p] + LAG * p for p in (c, chips - 1 - c) if p > 0)
        after += after % 2
        first = jnp.where(chip == c, after, first)
        last = max(last, after)

    def load_block(block, sem):
        return pltpu.make_async_copy(
            acts.at[:, pl.ds(pl.multiple_of(block * rows, rows), rows)], act_v.at[block], act_sem.at[sem]
        )

    def lanes(j):
        return pl.ds(pl.multiple_of(j * cols, cols), cols)

    bounds = [0, 2]
    while bounds[-1] < chunks:
        bounds.append(min(2 * bounds[-1], chunks))

    def grad_copy(k):
        at = pl.ds(bounds[k] * cols, (bounds[k + 1] - bounds[k]) * cols)
        return pltpu.make_async_copy(grads.at[:, at], grad_v.at[:, at], grad_sem.at[k])

    loads = [
        pltpu.make_async_copy(src.at[0], dst, load_sem.at[k])
        for k, (src, dst) in enumerate(((params, par_v), (estimate, est_v), (mixed, mix_v)))
    ]

    def to_sibling(at, recv_sem):
        return pltpu.make_async_remote_copy(
            src_ref=give.at[at] if at else give, dst_ref=got.at[at] if at else got,
            send_sem=pair_s, recv_sem=recv_sem,
            device_id={"mem": sibling}, device_id_type=MESH,
        )

    def half_copy(j, which):
        return to_sibling((j, which), half_r.at[j, which])

    def pair_copy(b, j):
        return to_sibling((b * (chunks // 2) + j,), pair_r.at[b, j % SLOTS])

    ring = line_r.shape[2]

    def line_copy(way, s, j):
        return pltpu.make_async_remote_copy(
            src_ref=line_out.at[way, s * chunks + j], dst_ref=line_in.at[way, s * chunks + j],
            send_sem=line_s.at[way, s, j % DEPTH], recv_sem=line_r.at[way, s, j % ring],
            device_id={"mem": line_to[way]}, device_id_type=MESH,
        )

    def to_group(src, dst, peer, send_sem, recv_sem, at):
        return pltpu.make_async_remote_copy(
            src_ref=src.at[at] if at else src, dst_ref=dst.at[at] if at else dst,
            send_sem=send_sem, recv_sem=recv_sem,
            device_id={"grp": peer}, device_id_type=MESH,
        )

    span = near_r.shape[0]
    relayed = chunks - DIRECT

    def near_copy(j):
        return to_group(own, near, near_to, near_s, near_r.at[j % span], (j,))

    def relay_copy(j):
        return to_group(near, far, onward, far_s, far_r.at[j % span], (j,))

    def far_copy(j):
        return to_group(own, far, far_to, far_s, far_r.at[span + j - relayed], (j,))

    def guarded(run, j, count, least=0):
        @pl.when(jnp.logical_and(j >= least, j < count))
        def _():
            run(j)

    lead_which = jnp.where(chip < pairs, 1, 0)
    lead = jnp.where(chip < pairs, chips - 1, 0)
    trail = chips - 1 - lead

    grad_copy(0).start()
    load_block(lead * 2 + other, 0).start()
    load_block(lead * 2 + core, 1).start()

    barrier = pltpu.get_barrier_semaphore()
    for peer in ({"mem": sibling}, {"grp": near_to}, {"grp": far_to}, {"grp": onward}, {"grp": backward}):
        pl.semaphore_signal(barrier, inc=1, device_id=peer, device_id_type=MESH)
    for way in (0, 1):
        @pl.when(place[way] < chips - 1)
        def _(way=way):
            pl.semaphore_signal(
                barrier, inc=1, device_id={"mem": line_to[way]}, device_id_type=MESH
            )
    greeted = 7 - jnp.where(chip == 0, 1, 0) - jnp.where(chip == chips - 1, 1, 0)

    load_block(trail * 2 + other, 2).start()
    load_block(trail * 2 + core, 3).start()
    grad_copy(1).start()

    def turn(block):
        act_t[block] = act_v[block].T

    def product(dest, parity, j):
        return jnp.dot(
            act_t[dest * 2 + parity],
            grad_v[:, pl.ds(pl.multiple_of(2 * j * cols, 2 * cols), 2 * cols)],
            preferred_element_type=f32,
        ).astype(bf16)

    def give_half(dest, which, j):
        give[j, which] = product(dest, other, j)
        half_copy(j, which).start()

    def keep_half(dest, which, j):
        mine[j, which] = product(dest, core, j)

    def multiply(b, j):
        i = b * (chunks // 2) + j
        if b == 0:
            for k in range(len(bounds) - 1):
                @pl.when(2 * j == bounds[k])
                def _(k=k):
                    grad_copy(k).wait()
        for which, dest in ((0, b), (1, chips - 1 - b)):
            give[i, which] = product(dest, other, j)
        pair_copy(b, j).start()
        for which, dest in ((0, b), (1, chips - 1 - b)):
            mine[i, which] = product(dest, core, j)

    def exchanged(b, j):
        pair_copy(b, j).wait_recv()

    def half_of(half):
        return pl.ds(half * cols, cols)

    def pair_sum(i, which, half):
        return mine[i, which, :, half_of(half)].astype(f32) + got[i, which, :, half_of(half)].astype(f32)

    def pass_on(way, s, j, half, least=0):
        far_dest = steps - s
        b = min(s, steps - s)
        which = (1 if far_dest >= pairs else 0) ^ way
        i = b * (chunks // 2) + j // 2
        slot = s * chunks + j

        @pl.when(jnp.logical_and(far_dest > place[way], jnp.logical_and(j >= least, j < chunks)))
        def _():
            @pl.when(j >= DEPTH)
            def _():
                line_copy(way, s, j - DEPTH).wait_send()

            @pl.when(place[way] == 0)
            def _():
                line_out[way, slot] = pair_sum(i, which, half).astype(bf16)

            @pl.when(place[way] > 0)
            def _():
                line_copy(way, s, j).wait_recv()
                line_out[way, slot] = (
                    pair_sum(i, which, half) + line_in[way, slot].astype(f32)
                ).astype(bf16)

            line_copy(way, s, j).start()

    weight_right = edges[g]
    weight_left = edges[lax.rem(g + groups - 1, groups)]
    weight_self = 1.0 - weight_left - weight_right
    weight_near = jnp.where(odd == 1, weight_left, weight_right)
    weight_far = jnp.where(odd == 1, weight_right, weight_left)
    blocks = exponents.shape[1]
    block_rows = rows // blocks
    own_which = jnp.where(chip >= pairs, 1, 0)
    own_block = jnp.where(chip >= pairs, chips - 1 - chip, chip)

    def compress(half, j):
        slot_of = [(steps - place[way]) * chunks + j for way in (0, 1)]
        @pl.when(j == 0)
        def _():
            for copy in loads:
                copy.wait()

        for way in (0, 1):
            @pl.when(place[way] == 0)
            def _(way=way):
                line_in[way, slot_of[way]] = jnp.zeros((rows, cols), bf16)

            @pl.when(place[way] > 0)
            def _(way=way):
                line_copy(way, steps - place[way], j).wait_recv()
        i = own_block * (chunks // 2) + j // 2
        for b in range(blocks):
            exponent = exponents[0, b]
            scale = (jnp.int32(1) << exponent).astype(f32)
            inverse = (jnp.int32(1) << (15 - exponent)).astype(f32) * (2.0 ** -15)
            at = pl.ds(b * block_rows, block_rows)
            gradient = (
                mine[i, own_which, at, half_of(half)].astype(f32)
                + got[i, own_which, at, half_of(half)].astype(f32)
                + line_in[0, slot_of[0], at, :].astype(f32)
                + line_in[1, slot_of[1], at, :].astype(f32)
            )
            stepped = par_v[at, lanes(j)] - factor * gradient
            levels = jnp.clip((stepped - est_v[at, lanes(j)]) * inverse, -1.0, 1.0).astype(bf16)
            own[j, at, :] = (levels.astype(f32) * scale).astype(bf16)
            out_params[0, at, lanes(j)] = stepped
        @pl.when(j >= relayed)
        def _():
            far_copy(j).start()

        near_copy(j).start()
        compressed = own[j].astype(f32)
        out_estimate[0, :, lanes(j)] = est_v[:, lanes(j)] + compressed
        out_mixed[0, :, lanes(j)] = mix_v[:, lanes(j)] + weight_self * compressed

    def forward(j):
        near_copy(j).wait_recv()

        @pl.when(j < relayed)
        def _():
            relay_copy(j).start()

    def finish(j):
        @pl.when(j < relayed)
        def _():
            relay_copy(j).wait_recv()

        @pl.when(j >= relayed)
        def _():
            far_copy(j).wait_recv()

        total = (
            out_mixed[0, :, lanes(j)] + weight_near * near[j].astype(f32) + weight_far * far[j].astype(f32)
        )
        out_mixed[0, :, lanes(j)] = total
        out_params[0, :, lanes(j)] = out_params[0, :, lanes(j)] + mixing_rate * (
            total - out_estimate[0, :, lanes(j)]
        )

    def head(j):
        for way in (0, 1):
            for half in (0, 1):
                @pl.when(place[way] == 0)
                def _(way=way, half=half):
                    pass_on(way, 0, jnp.int32(2 * j + half), half)

    with jax.named_scope("lead"):
        grad_copy(0).wait()
        load_block(lead * 2 + other, 0).wait()
        turn(lead * 2 + other)
        give[0, lead_which] = product(lead, other, 0)
    with jax.named_scope("barrier"):
        pl.semaphore_wait(barrier, greeted)
        half_copy(0, lead_which).start()
    with jax.named_scope("lead2"):
        load_block(lead * 2 + core, 1).wait()
        turn(lead * 2 + core)
        keep_half(lead, lead_which, 0)
        half_copy(0, lead_which).wait_recv()
        head(0)
    with jax.named_scope("lead3"):
        grad_copy(1).wait()
        give_half(lead, lead_which, 1)
        keep_half(lead, lead_which, 1)
        for block in range(2, members - 2):
            load_block(block, 4).start()
        for k in range(2, len(bounds) - 1):
            grad_copy(k).start()
    with jax.named_scope("trail"):
        load_block(trail * 2 + other, 2).wait()
        turn(trail * 2 + other)
        for j in (0, 1):
            give_half(trail, 1 - lead_which, j)
        half_copy(1, lead_which).wait_recv()
        head(1)
        load_block(trail * 2 + core, 3).wait()
        turn(trail * 2 + core)
        for j in (0, 1):
            keep_half(trail, 1 - lead_which, j)
        for copy in loads:
            copy.start()
        for j in (0, 1):
            half_copy(j, 1 - lead_which).wait_recv()

    def turn_four(b):
        if members > 4:
            @pl.when(b == 1)
            def _():
                pltpu.make_async_copy(
                    act_v.at[pl.ds(2, members - 4)], act_v.at[pl.ds(2, members - 4)], act_sem.at[4]
                ).wait()

            for parity in (0, 1):
                for dest in (b, chips - 1 - b):
                    turn(dest * 2 + parity)

    def body(d, carry):
        for half in (0, 1):
            r = 2 * d + half
            for s in range(steps):
                odd_half = (half - begin[s]) % 2
                with jax.named_scope(f"pass{s}"):
                    if s < pairs and odd_half == 0:
                        guarded(
                            functools.partial(exchanged, s),
                            (r - begin[s]) // 2, chunks // 2, 0 if s else SPLIT,
                        )
                    for way in (0, 1):
                        least = 0 if s else jnp.where(place[way] == 0, 2 * SPLIT, 0)
                        pass_on(way, s, r - LAG * place[way] - begin[s], odd_half, least)
                if half == 0 and s == 0:
                    with jax.named_scope("turn"):
                        guarded(turn_four, d, pairs, 1)
                if half == 0 and s < pairs:
                    with jax.named_scope(f"mult{s}"):
                        guarded(
                            functools.partial(multiply, s), d - s - 1 if s else d + 1, chunks // 2
                        )
            with jax.named_scope("compress"):
                guarded(functools.partial(compress, half), r - first, chunks)
            with jax.named_scope("forward"):
                guarded(forward, r - first - RELAY, chunks)
            with jax.named_scope("finish"):
                guarded(finish, r - first - GOSSIP, chunks)
        return carry

    lax.fori_loop(1, (chunks + last + GOSSIP + 1) // 2, body, 0)

    with jax.named_scope("drain"):
        to_sibling((), half_r.at[0, 0]).wait_send()
        for way in (0, 1):
            for s in range(steps):
                @pl.when(steps - s > place[way])
                def _(way=way, s=s):
                    for k in range(DEPTH):
                        line_copy(way, s, chunks - 1 - k).wait_send()
        to_group(own, near, near_to, near_s, near_r.at[0], ()).wait_send()
        to_group(own, far, far_to, far_s, far_r.at[0], ()).wait_send()


def flush(pieces, *refs):
    sources, targets, sems = refs[:3], refs[3:6], refs[6]
    rows = sources[0].shape[1] // pieces
    copies = [
        pltpu.make_async_copy(
            sources[a].at[:, pl.ds(k * rows, rows)], targets[a].at[:, pl.ds(k * rows, rows)], sems.at[a, k]
        )
        for k in range(pieces)
        for a in range(3)
    ]
    for copy in copies:
        copy.start()
    for copy in copies:
        copy.wait()


def on_device(members, groups, params, estimate, mixed, acts, grads, exponents, edges):
    rows, width = params.shape[1:]
    tokens = acts.shape[0]
    chunks = CHUNKS
    cols = width // chunks
    chips = members // 2
    items = chips // 2 * chunks // 2
    slots = (chips - 1) * chunks
    ring = min(chunks, LAG * (chips - 1) + 2)
    span = RING if groups <= 4 else chunks
    factor = step_size / math.sqrt(members * tokens)
    cfg = (members, groups, chunks, rows, width, tokens, factor)
    wide = (chunks, rows, cols)
    tall = (items, 2, rows, 2 * cols)
    dma = pltpu.SemaphoreType.DMA
    any_spec = pl.BlockSpec(memory_space=pl.ANY)
    smem = pl.BlockSpec(memory_space=pltpu.SMEM)
    vmem = pl.BlockSpec(memory_space=pltpu.VMEM)
    results = pl.pallas_call(
        functools.partial(kernel, cfg),
        out_shape=[pltpu.VMEM(params.shape, f32)] * 3,
        in_specs=[any_spec] * 5 + [smem] * 2,
        out_specs=[vmem] * 3,
        scratch_shapes=[
            pltpu.VMEM((members, tokens, rows), bf16),
            pltpu.VMEM((members, rows, tokens), bf16),
            pltpu.VMEM((tokens, width), bf16),
            *[pltpu.VMEM((rows, width), f32)] * 3,
            *[pltpu.VMEM(tall, bf16)] * 3,
            pltpu.VMEM((2, slots, rows, cols), bf16),
            pltpu.VMEM((2, slots + chunks, rows, cols), bf16),
            *[pltpu.VMEM(wide, bf16)] * 3,
            dma((5,)), dma((chunks.bit_length(),)), dma((3,)),
            dma, dma((SPLIT, 2)), dma((chips // 2, SLOTS)),
            dma((2, chips - 1, DEPTH)), dma((2, chips - 1, ring)),
            dma, dma((span,)), dma, dma((span + DIRECT,)),
        ],
        compiler_params=pltpu.CompilerParams(
            collective_id=0, has_side_effects=True, vmem_limit_bytes=53 * 1024 * 1024
        ),
    )(params, estimate, mixed, acts, grads, exponents, edges)
    pieces = math.gcd(PIECES, rows // 8)
    return pl.pallas_call(
        functools.partial(flush, pieces),
        out_shape=[jax.ShapeDtypeStruct(params.shape, f32)] * 3,
        in_specs=[vmem] * 3,
        out_specs=[any_spec] * 3,
        scratch_shapes=[dma((3, pieces))],
        compiler_params=pltpu.CompilerParams(vmem_limit_bytes=1024 * 1024),
    )(*results)


def solution(mesh):
    shard = P("grp", "mem", None)
    tokens = P(("grp", "mem"), None)
    return jax.shard_map(
        functools.partial(on_device, mesh.shape["mem"], mesh.shape["grp"]),
        mesh=mesh,
        in_specs=(shard, shard, shard, tokens, tokens, P("grp", "mem"), P()),
        out_specs=(shard, shard, shard),
        check_vma=False,
    )
```

time: 93.1 us -> 87.8 us (0.943)
  local copies, waits for them, and re-layouts: 3.96 us -> 0 us
  Pallas kernels: 88.2 us -> 87 us
    pallas_call x1, Pallas kernels: 88.2 us -> 84.2 us  [on_device(): pl.pallas_call(functools.partial(kernel, cfg), out_shape=[pltpu.VMEM(para...]
    unnamed x3 -> x0, local copies, waits for them, and re-layouts: 3.96 us -> none
    pallas_call x0 -> x1, Pallas kernels: none -> 2.75 us  [on_device(): pl.pallas_call(functools.partial(flush, pieces), out_shape=[jax.ShapeDtyp...]
where the time goes in v1:
time: 87.8 us; the launch traced here: 87.6 us
  Pallas kernels  87 us (99%)
    pallas_call x1, Pallas kernels, on_device(): pl.pallas_call(functools.partial(kernel, cfg), out_shape=[pltpu.VMEM(para...  84.2 us
    pallas_call x1, Pallas kernels, on_device(): pl.pallas_call(functools.partial(flush, pieces), out_shape=[jax.ShapeDtyp...  2.75 us

profile of v1, /device:TPU:16, one launch (start us, length us, event | category | flops | bytes accessed | tf_op | source)
XLA Modules:
  0.0 87.6 jit_solution(9807866056382979907)
XLA Ops:
  0.6 84.2 %shard_map.94 = (f32[1,256,2048]{2,1,0:T(8,128)S(1)}, f32[1,256,2048]{2,1,0:T(8,128)S(1)}, f32[1,256,2048]{2,1,0:T(8,128)S(1)}) custom-call(f32[1,256,2048]{2,1,0:T(8,128)} %params.1, f32[1,256,2048]{2,1,0:T(8,128)} %estimate.1, f32[1,256,2048]{2,1,0:T(8,128)} %mixed.1, bf16[1024,2048]{1,0:T(8,128)(2,1)} %acts.1, bf16[1024,2048]{1,0:T(8,128)(2,1)} %grads.1, ...), custom_call_target="tpu_custom_call" | custom-call | tf_op jit(solution)/shard_map/pallas_call | solution.py:433
  84.9 2.8 %shard_map.95 = (f32[1,256,2048]{2,1,0:T(8,128)}, f32[1,256,2048]{2,1,0:T(8,128)}, f32[1,256,2048]{2,1,0:T(8,128)}) custom-call(f32[1,256,2048]{2,1,0:T(8,128)S(1)} %get-tuple-element.6.refs_0_, f32[1,256,2048]{2,1,0:T(8,128)S(1)} %get-tuple-element.7.refs_1_, f32[1,256,2048]{2,1,0:T(8,128)S(1)} %get-tuple-element.8.refs_2_), custom_call_target="tpu_custom_call" | custom-call | tf_op jit(solution)/shard_map/pallas_call | solution.py:457

commit v2 on v1

v2 whole, which is shorter than its diff:
```python
import functools
import math

import jax
import jax.numpy as jnp
from jax import lax
from jax.experimental import pallas as pl
from jax.experimental.pallas import tpu as pltpu
from jax.sharding import PartitionSpec as P

step_size = 0.5
mixing_rate = 0.4
CHUNKS = 16
LAG = 1
RELAY = 1
GOSSIP = 3
DIRECT = 1
PIECES = 4
SLOTS = 4
RING = 8
MESH = pl.DeviceIdType.MESH
f32 = jnp.float32
bf16 = jnp.bfloat16


def kernel(
    cfg,
    params, estimate, mixed, acts, grads, exponents, edges,
    out_params, out_estimate, out_mixed,
    act_v, act_t, grad_v, par_v, est_v, mix_v,
    mine, give, got, line_out, line_in, own, near, far,
    act_sem, grad_sem, load_sem,
    pair_s, half_r, pair_r, line_s, line_r, near_s, near_r, far_s, far_r,
):
    members, groups, chunks, rows, width, tokens, factor = cfg
    chips = members // 2
    pairs = chips // 2
    steps = chips - 1
    cols = width // chunks
    g = lax.axis_index("grp")
    m = lax.axis_index("mem")
    chip, core = m // 2, m % 2
    other = 1 - core
    sibling = chip * 2 + other
    upper = jnp.where(chip < pairs, 0, 1)
    edge = jnp.where(chip < pairs, chip, chips - 1 - chip)
    inward = lax.rem(chip + chips + 1 - 2 * upper, chips) * 2 + core
    outward = lax.rem(chip + chips - 1 + 2 * upper, chips) * 2 + core
    ways = ((upper, edge, inward), (1 - upper, chips - 1 - edge, outward))
    odd = g % 2
    near_to = lax.rem(g + groups + 1 - 2 * odd, groups)
    far_to = lax.rem(g + groups - 1 + 2 * odd, groups)
    onward = lax.rem(g + groups + 2 - 4 * odd, groups)
    backward = lax.rem(g + groups - 2 + 4 * odd, groups)

    begin = [2 * s for s in range(pairs)]
    for s in range(pairs, steps):
        begin.append(begin[-1] + 1)
    first = max(begin[steps - p] + LAG * p for p in range(1, chips))
    first += first % 2

    def load_block(block, sem):
        return pltpu.make_async_copy(
            acts.at[:, pl.ds(pl.multiple_of(block * rows, rows), rows)], act_v.at[block], act_sem.at[sem]
        )

    def lanes(j):
        return pl.ds(pl.multiple_of(j * cols, cols), cols)

    bounds = [0, 2]
    while bounds[-1] < chunks:
        bounds.append(min(2 * bounds[-1], chunks))

    def grad_copy(k):
        at = pl.ds(bounds[k] * cols, (bounds[k + 1] - bounds[k]) * cols)
        return pltpu.make_async_copy(grads.at[:, at], grad_v.at[:, at], grad_sem.at[k])

    loads = [
        pltpu.make_async_copy(src.at[0], dst, load_sem.at[k])
        for k, (src, dst) in enumerate(((params, par_v), (estimate, est_v), (mixed, mix_v)))
    ]

    def to_sibling(at, recv_sem):
        return pltpu.make_async_remote_copy(
            src_ref=give.at[at] if at else give, dst_ref=got.at[at] if at else got,
            send_sem=pair_s, recv_sem=recv_sem,
            device_id={"mem": sibling}, device_id_type=MESH,
        )

    half_at = (0, 1, chunks // 2)
    half_of_width = (0, 1, 0)

    def half_copy(h, which):
        return to_sibling((half_at[h], which), half_r.at[h, which])

    def pair_copy(b, j):
        return to_sibling((b * (chunks // 2) + j,), pair_r.at[b, j % SLOTS])

    ring = line_r.shape[2]

    def line_copy(way, s, j):
        return pltpu.make_async_remote_copy(
            src_ref=line_out.at[way[0], s * chunks + j], dst_ref=line_in.at[way[0], s * chunks + j],
            send_sem=line_s.at[way[0], s, jnp.where(way[1] == 0, j % 2, 0)], recv_sem=line_r.at[way[0], s, j % ring],
            device_id={"mem": way[2]}, device_id_type=MESH,
        )

    def to_group(src, dst, peer, send_sem, recv_sem, at):
        return pltpu.make_async_remote_copy(
            src_ref=src.at[at] if at else src, dst_ref=dst.at[at] if at else dst,
            send_sem=send_sem, recv_sem=recv_sem,
            device_id={"grp": peer}, device_id_type=MESH,
        )

    span = near_r.shape[0]
    relayed = chunks - DIRECT

    def near_copy(j):
        return to_group(own, near, near_to, near_s, near_r.at[j % span], (j,))

    def relay_copy(j):
        return to_group(near, far, onward, far_s, far_r.at[j % span], (j,))

    def far_copy(j):
        return to_group(own, far, far_to, far_s, far_r.at[span + j - relayed], (j,))

    def guarded(run, j, count, least=0):
        @pl.when(jnp.logical_and(j >= least, j < count))
        def _():
            run(j)

    lead_which = 1 - upper
    lead = jnp.where(chip < pairs, chips - 1, 0)
    trail = chips - 1 - lead
    lead_next = jnp.where(chip < pairs, chips - 2, 1)
    trail_next = chips - 1 - lead_next

    grad_copy(0).start()
    load_block(lead * 2 + other, 0).start()

    barrier = pltpu.get_barrier_semaphore()
    for peer in ({"mem": sibling}, {"grp": near_to}, {"grp": far_to}, {"grp": onward}, {"grp": backward}):
        pl.semaphore_signal(barrier, inc=1, device_id=peer, device_id_type=MESH)
    pl.semaphore_signal(barrier, inc=1, device_id={"mem": inward}, device_id_type=MESH)

    @pl.when(edge > 0)
    def _():
        pl.semaphore_signal(barrier, inc=1, device_id={"mem": outward}, device_id_type=MESH)

    greeted = 7 - jnp.where(edge == 0, 1, 0)
    load_block(lead * 2 + core, 1).start()
    grad_copy(1).start()
    for parity, sem in ((other, 2), (core, 3)):
        load_block(lead_next * 2 + parity, sem).start()
    for parity, sem in ((other, 4), (core, 5)):
        for dest in (trail, trail_next):
            load_block(dest * 2 + parity, sem).start()

    def turn(block):
        act_t[block] = act_v[block].T

    def product(dest, parity, j):
        return jnp.dot(
            act_t[dest * 2 + parity],
            grad_v[:, pl.ds(pl.multiple_of(2 * j * cols, 2 * cols), 2 * cols)],
            preferred_element_type=f32,
        ).astype(bf16)

    def put(ref, i, which, value):
        for half in (0, 1):
            ref[i, which, half] = value[:, half * cols : (half + 1) * cols]

    def give_half(dest, which, h):
        put(give, half_at[h], which, product(dest, other, half_of_width[h]))
        half_copy(h, which).start()

    def keep_half(dest, which, h):
        put(mine, half_at[h], which, product(dest, core, half_of_width[h]))

    def multiply(b, j):
        i = b * (chunks // 2) + j
        if b == 0:
            for k in range(len(bounds) - 1):
                @pl.when(2 * j == bounds[k])
                def _(k=k):
                    grad_copy(k).wait()
        for which, dest in ((0, b), (1, chips - 1 - b)):
            put(give, i, which, product(dest, other, j))
        pair_copy(b, j).start()
        for which, dest in ((0, b), (1, chips - 1 - b)):
            put(mine, i, which, product(dest, core, j))

    def exchanged(b, j):
        pair_copy(b, j).wait_recv()

    def pair_sum(i, which, half):
        return mine[i, which, half].astype(f32) + got[i, which, half].astype(f32)

    def pass_on(way, s, j, least=0):
        far_dest = steps - s
        b = min(s, steps - s)
        which = 1 - way[0] if far_dest >= pairs else way[0]
        i = b * (chunks // 2) + j // 2
        slot = s * chunks + j

        @pl.when(jnp.logical_and(far_dest > way[1], jnp.logical_and(j >= least, j < chunks)))
        def _():
            @pl.when(way[1] == 0)
            def _():
                line_out[way[0], slot] = pair_sum(i, which, j % 2).astype(bf16)

            @pl.when(way[1] > 0)
            def _():
                line_copy(way, s, j).wait_recv()
                line_out[way[0], slot] = (
                    pair_sum(i, which, j % 2) + line_in[way[0], slot].astype(f32)
                ).astype(bf16)

            line_copy(way, s, j).start()

    def sent(s, j):
        line_copy(ways[0], s, j).wait_send()

    def pace(s, r):
        j = r - begin[s]

        @pl.when(jnp.logical_and(r > (4 if s == 0 else 3), jnp.logical_and(j >= 1, j < chunks)))
        def _():
            sent(s, j - 1)

        early = {0: ((4, 1, 0),), 1: ((2, 0, 1), (3, 0, 2)), 2: ((3, 0, 3),)}.get(s, ())
        for at, step, chunk in early:
            @pl.when(r == at)
            def _(step=step, chunk=chunk):
                sent(step, chunk)

    weight_right = edges[g]
    weight_left = edges[lax.rem(g + groups - 1, groups)]
    weight_self = 1.0 - weight_left - weight_right
    weight_near = jnp.where(odd == 1, weight_left, weight_right)
    weight_far = jnp.where(odd == 1, weight_right, weight_left)
    blocks = exponents.shape[1]
    block_rows = rows // blocks

    def compress(j):
        slot_of = [(steps - way[1]) * chunks + j for way in ways]

        @pl.when(j == 0)
        def _():
            for copy in loads:
                copy.wait()

        line_copy(ways[1], steps - ways[1][1], j).wait_recv()

        @pl.when(edge == 0)
        def _():
            line_in[upper, slot_of[0]] = jnp.zeros((rows, cols), bf16)

        @pl.when(edge > 0)
        def _():
            line_copy(ways[0], steps - edge, j).wait_recv()

        i = edge * (chunks // 2) + j // 2
        for b in range(blocks):
            exponent = exponents[0, b]
            scale = (jnp.int32(1) << exponent).astype(f32)
            inverse = (jnp.int32(1) << (15 - exponent)).astype(f32) * (2.0 ** -15)
            at = pl.ds(b * block_rows, block_rows)
            gradient = (
                mine[i, upper, j % 2, at, :].astype(f32)
                + got[i, upper, j % 2, at, :].astype(f32)
                + line_in[upper, slot_of[0], at, :].astype(f32)
                + line_in[1 - upper, slot_of[1], at, :].astype(f32)
            )
            stepped = par_v[at, lanes(j)] - factor * gradient
            levels = jnp.clip((stepped - est_v[at, lanes(j)]) * inverse, -1.0, 1.0).astype(bf16)
            own[j, at, :] = (levels.astype(f32) * scale).astype(bf16)
            out_params[0, at, lanes(j)] = stepped
        @pl.when(j >= relayed)
        def _():
            far_copy(j).start()

        near_copy(j).start()
        compressed = own[j].astype(f32)
        out_estimate[0, :, lanes(j)] = est_v[:, lanes(j)] + compressed
        out_mixed[0, :, lanes(j)] = mix_v[:, lanes(j)] + weight_self * compressed

    def forward(j):
        near_copy(j).wait_recv()

        @pl.when(j < relayed)
        def _():
            relay_copy(j).start()

    def finish(j):
        @pl.when(j < relayed)
        def _():
            relay_copy(j).wait_recv()

        @pl.when(j >= relayed)
        def _():
            far_copy(j).wait_recv()

        total = (
            out_mixed[0, :, lanes(j)] + weight_near * near[j].astype(f32) + weight_far * far[j].astype(f32)
        )
        out_mixed[0, :, lanes(j)] = total
        out_params[0, :, lanes(j)] = out_params[0, :, lanes(j)] + mixing_rate * (
            total - out_estimate[0, :, lanes(j)]
        )

    def head(s, j):
        @pl.when(edge == 0)
        def _():
            for half in (0, 1):
                if j == 1 and half == 0:
                    sent(0, 0)
                pass_on(ways[0], s, jnp.int32(2 * j + half))

    with jax.named_scope("lead"):
        grad_copy(0).wait()
        load_block(lead * 2 + other, 0).wait()
    with jax.named_scope("lead1"):
        turn(lead * 2 + other)
        put(give, 0, lead_which, product(lead, other, 0))
    with jax.named_scope("barrier"):
        pl.semaphore_wait(barrier, greeted)
        half_copy(0, lead_which).start()
    with jax.named_scope("lead2"):
        load_block(lead * 2 + core, 1).wait()
        turn(lead * 2 + core)
        keep_half(lead, lead_which, 0)
        half_copy(0, lead_which).wait_recv()
        head(0, 0)
    with jax.named_scope("lead3"):
        grad_copy(1).wait()
        give_half(lead, lead_which, 1)
        keep_half(lead, lead_which, 1)
        load_block(lead_next * 2 + other, 2).wait()
        turn(lead_next * 2 + other)
        give_half(lead_next, lead_which, 2)
        load_block(lead_next * 2 + core, 3).wait()
        turn(lead_next * 2 + core)
        keep_half(lead_next, lead_which, 2)
        for block in range(4, members - 4):
            load_block(block, 6).start()
        for k in range(2, len(bounds) - 1):
            grad_copy(k).start()

    def both_trails(parity, sem):
        block = act_v.at[pl.ds(0, 2)]
        pltpu.make_async_copy(block, block, act_sem.at[sem]).wait()
        turn(trail * 2 + parity)
        turn(trail_next * 2 + parity)

    with jax.named_scope("trail"):
        both_trails(other, 4)
        give_half(trail, 1 - lead_which, 0)
        half_copy(1, lead_which).wait_recv()
        head(0, 1)
        give_half(trail, 1 - lead_which, 1)
        give_half(trail_next, 1 - lead_which, 2)
    with jax.named_scope("trail2"):
        both_trails(core, 5)
        for h, dest in enumerate((trail, trail, trail_next)):
            keep_half(dest, 1 - lead_which, h)
        for copy in loads:
            copy.start()
        half_copy(2, lead_which).wait_recv()
        head(1, 0)
        for h in range(3):
            half_copy(h, 1 - lead_which).wait_recv()

    def turn_four(b):
        if members > 8:
            @pl.when(b == 2)
            def _():
                block = act_v.at[pl.ds(4, members - 8)]
                pltpu.make_async_copy(block, block, act_sem.at[6]).wait()

            for parity in (0, 1):
                for dest in (b, chips - 1 - b):
                    turn(dest * 2 + parity)

    sent_early = (4, 2)
    ready = [2, 1] + [0] * pairs

    def body(d, carry):
        for half in (0, 1):
            r = 2 * d + half
            for s in range(steps):
                odd_half = (half - begin[s]) % 2
                with jax.named_scope(f"pass{s}"):
                    if s < pairs and odd_half == 0:
                        guarded(
                            functools.partial(exchanged, s),
                            (r - begin[s]) // 2, chunks // 2, ready[s],
                        )
                    @pl.when(edge == 0)
                    def _(s=s, r=r):
                        pace(s, r)

                    for way in ways:
                        least = jnp.where(way[1] == 0, sent_early[s], 0) if s < 2 else 0
                        pass_on(way, s, r - LAG * way[1] - begin[s], least)
                if half == 0 and s == 0 and pairs > 2:
                    guarded(turn_four, d + 1, pairs, 2)
                if half == 0 and s < pairs:
                    with jax.named_scope(f"mult{s}"):
                        guarded(functools.partial(multiply, s), d + 1 - s, chunks // 2, ready[s])
            with jax.named_scope("compress"):
                guarded(compress, r - first, chunks)
            with jax.named_scope("forward"):
                guarded(forward, r - first - RELAY, chunks)
            with jax.named_scope("finish"):
                guarded(finish, r - first - GOSSIP, chunks)
        return carry

    lax.fori_loop(0, (chunks + first + GOSSIP + 1) // 2, body, 0)

    with jax.named_scope("drain"):
        to_sibling((), half_r.at[0, 0]).wait_send()
        for way in ways:
            for s in range(steps):
                @pl.when(jnp.logical_and(way[1] > 0, steps - s > way[1]))
                def _(way=way, s=s):
                    whole = line_out.at[way[0], pl.ds(s * chunks, chunks)]
                    pltpu.make_async_remote_copy(
                        src_ref=whole, dst_ref=whole, send_sem=line_s.at[way[0], s, 0],
                        recv_sem=line_r.at[way[0], s, 0],
                        device_id={"mem": way[2]}, device_id_type=MESH,
                    ).wait_send()

        @pl.when(edge == 0)
        def _():
            for s in range(steps):
                sent(s, chunks - 1)

        to_group(own, near, near_to, near_s, near_r.at[0], ()).wait_send()
        to_group(own, far, far_to, far_s, far_r.at[0], ()).wait_send()


def flush(pieces, *refs):
    sources, targets, sems = refs[:3], refs[3:6], refs[6]
    rows = sources[0].shape[1] // pieces
    copies = [
        pltpu.make_async_copy(
            sources[a].at[:, pl.ds(k * rows, rows)], targets[a].at[:, pl.ds(k * rows, rows)], sems.at[a, k]
        )
        for k in range(pieces)
        for a in range(3)
    ]
    for copy in copies:
        copy.start()
    for copy in copies:
        copy.wait()


def on_device(members, groups, params, estimate, mixed, acts, grads, exponents, edges):
    rows, width = params.shape[1:]
    tokens = acts.shape[0]
    chunks = CHUNKS
    cols = width // chunks
    chips = members // 2
    items = chips // 2 * chunks // 2
    slots = (chips - 1) * chunks
    ring = 6 if chips <= 4 else chunks
    span = RING if groups <= 4 else chunks
    factor = step_size / math.sqrt(members * tokens)
    cfg = (members, groups, chunks, rows, width, tokens, factor)
    wide = (chunks, rows, cols)
    tall = (items, 2, 2, rows, cols)
    dma = pltpu.SemaphoreType.DMA
    any_spec = pl.BlockSpec(memory_space=pl.ANY)
    smem = pl.BlockSpec(memory_space=pltpu.SMEM)
    vmem = pl.BlockSpec(memory_space=pltpu.VMEM)
    results = pl.pallas_call(
        functools.partial(kernel, cfg),
        out_shape=[pltpu.VMEM(params.shape, f32)] * 3,
        in_specs=[any_spec] * 5 + [smem] * 2,
        out_specs=[vmem] * 3,
        scratch_shapes=[
            pltpu.VMEM((members, tokens, rows), bf16),
            pltpu.VMEM((members, rows, tokens), bf16),
            pltpu.VMEM((tokens, width), bf16),
            *[pltpu.VMEM((rows, width), f32)] * 3,
            *[pltpu.VMEM(tall, bf16)] * 3,
            pltpu.VMEM((2, slots, rows, cols), bf16),
            pltpu.VMEM((2, slots + chunks, rows, cols), bf16),
            *[pltpu.VMEM(wide, bf16)] * 3,
            dma((7,)), dma((chunks.bit_length(),)), dma((3,)),
            dma, dma((3, 2)), dma((chips // 2, SLOTS)),
            dma((2, chips - 1, 2)), dma((2, chips - 1, ring)),
            dma, dma((span,)), dma, dma((span + DIRECT,)),
        ],
        compiler_params=pltpu.CompilerParams(
            collective_id=0, has_side_effects=True, vmem_limit_bytes=53 * 1024 * 1024
        ),
    )(params, estimate, mixed, acts, grads, exponents, edges)
    pieces = math.gcd(PIECES, rows // 8)
    return pl.pallas_call(
        functools.partial(flush, pieces),
        out_shape=[jax.ShapeDtypeStruct(params.shape, f32)] * 3,
        in_specs=[vmem] * 3,
        out_specs=[any_spec] * 3,
        scratch_shapes=[dma((3, pieces))],
        compiler_params=pltpu.CompilerParams(vmem_limit_bytes=1024 * 1024),
    )(*results)


def solution(mesh):
    shard = P("grp", "mem", None)
    tokens = P(("grp", "mem"), None)
    return jax.shard_map(
        functools.partial(on_device, mesh.shape["mem"], mesh.shape["grp"]),
        mesh=mesh,
        in_specs=(shard, shard, shard, tokens, tokens, P("grp", "mem"), P()),
        out_specs=(shard, shard, shard),
        check_vma=False,
    )
```

time: 87.8 us -> 85.1 us (0.969)
  Pallas kernels: 87 us -> 84.2 us
    pallas_call x1, Pallas kernels: 84.2 us -> 81.5 us  [on_device(): pl.pallas_call(functools.partial(kernel, cfg), out_shape=[pltpu.VMEM(para...]
where the time goes in v2:
time: 85.1 us; the launch traced here: 84.8 us
  Pallas kernels  84.2 us (99%)
    pallas_call x1, Pallas kernels, on_device(): pl.pallas_call(functools.partial(kernel, cfg), out_shape=[pltpu.VMEM(para...  81.5 us
    pallas_call x1, Pallas kernels, on_device(): pl.pallas_call(functools.partial(flush, pieces), out_shape=[jax.ShapeDtyp...  2.75 us

profile of v2, /device:TPU:16, one launch (start us, length us, event | category | flops | bytes accessed | tf_op | source)
XLA Modules:
  0.0 84.8 jit_solution(17646198152448319647)
XLA Ops:
  0.6 81.5 %shard_map.94 = (f32[1,256,2048]{2,1,0:T(8,128)S(1)}, f32[1,256,2048]{2,1,0:T(8,128)S(1)}, f32[1,256,2048]{2,1,0:T(8,128)S(1)}) custom-call(f32[1,256,2048]{2,1,0:T(8,128)} %params.1, f32[1,256,2048]{2,1,0:T(8,128)} %estimate.1, f32[1,256,2048]{2,1,0:T(8,128)} %mixed.1, bf16[1024,2048]{1,0:T(8,128)(2,1)} %acts.1, bf16[1024,2048]{1,0:T(8,128)(2,1)} %grads.1, ...), custom_call_target="tpu_custom_call" | custom-call | tf_op jit(solution)/shard_map/pallas_call | solution.py:477
  82.1 2.8 %shard_map.95 = (f32[1,256,2048]{2,1,0:T(8,128)}, f32[1,256,2048]{2,1,0:T(8,128)}, f32[1,256,2048]{2,1,0:T(8,128)}) custom-call(f32[1,256,2048]{2,1,0:T(8,128)S(1)} %get-tuple-element.6.refs_0_, f32[1,256,2048]{2,1,0:T(8,128)S(1)} %get-tuple-element.7.refs_1_, f32[1,256,2048]{2,1,0:T(8,128)S(1)} %get-tuple-element.8.refs_2_), custom_call_target="tpu_custom_call" | custom-call | tf_op jit(solution)/shard_map/pallas_call | solution.py:501

commit v3 on v2

--- a/solution.py
+++ b/solution.py
@@ -13,11 +13,13 @@
 CHUNKS = 16
 LAG = 1
 RELAY = 1
-GOSSIP = 3
+GOSSIP = 2
 DIRECT = 1
 PIECES = 4
-SLOTS = 4
-RING = 8
+SLOTS = 2
+STEP = 1
+RING = 6
+PARTS = 2
 MESH = pl.DeviceIdType.MESH
 f32 = jnp.float32
 bf16 = jnp.bfloat16
@@ -55,9 +57,8 @@
 
     begin = [2 * s for s in range(pairs)]
     for s in range(pairs, steps):
-        begin.append(begin[-1] + 1)
+        begin.append(begin[-1] + STEP)
     first = max(begin[steps - p] + LAG * p for p in range(1, chips))
-    first += first % 2
 
     def load_block(block, sem):
         return pltpu.make_async_copy(
@@ -115,14 +116,17 @@
     span = near_r.shape[0]
     relayed = chunks - DIRECT
 
-    def near_copy(j):
-        return to_group(own, near, near_to, near_s, near_r.at[j % span], (j,))
-
-    def relay_copy(j):
-        return to_group(near, far, onward, far_s, far_r.at[j % span], (j,))
+    def part_of(j, k):
+        return (j, pl.ds(k * (rows // PARTS), rows // PARTS))
+
+    def near_copy(j, k):
+        return to_group(own, near, near_to, near_s, near_r.at[j % span, k], part_of(j, k))
+
+    def relay_copy(j, k):
+        return to_group(near, far, onward, far_s, far_r.at[j % span, k], part_of(j, k))
 
     def far_copy(j):
-        return to_group(own, far, far_to, far_s, far_r.at[span + j - relayed], (j,))
+        return to_group(own, far, far_to, far_s, far_r.at[span + j - relayed, 0], (j,))
 
     def guarded(run, j, count, least=0):
         @pl.when(jnp.logical_and(j >= least, j < count))
@@ -221,15 +225,22 @@
     def sent(s, j):
         line_copy(ways[0], s, j).wait_send()
 
+    late = begin == [0, 2, 3]
+
     def pace(s, r):
         j = r - begin[s]
 
-        @pl.when(jnp.logical_and(r > (4 if s == 0 else 3), jnp.logical_and(j >= 1, j < chunks)))
+        @pl.when(jnp.logical_and(r > (4 if s == 0 else 3), jnp.logical_and(j >= 1, (r if late else j) < chunks)))
         def _():
             sent(s, j - 1)
 
-        early = {0: ((4, 1, 0),), 1: ((2, 0, 1), (3, 0, 2)), 2: ((3, 0, 3),)}.get(s, ())
-        for at, step, chunk in early:
+        turns = {0: ((4, 1, 0),), 1: ((2, 0, 1), (3, 0, 2)), 2: ((3, 0, 3),)}.get(s, ())
+        if late:
+            turns += {
+                1: ((chunks, 0, chunks - 1), (chunks + 1, 2, chunks - 4)),
+                2: ((chunks, 1, chunks - 3), (chunks + 1, 1, chunks - 2), (chunks + 2, 2, chunks - 3)),
+            }.get(s, ())
+        for at, step, chunk in turns:
             @pl.when(r == at)
             def _(step=step, chunk=chunk):
                 sent(step, chunk)
@@ -280,22 +291,25 @@
         def _():
             far_copy(j).start()
 
-        near_copy(j).start()
+        for k in range(PARTS):
+            near_copy(j, k).start()
         compressed = own[j].astype(f32)
         out_estimate[0, :, lanes(j)] = est_v[:, lanes(j)] + compressed
         out_mixed[0, :, lanes(j)] = mix_v[:, lanes(j)] + weight_self * compressed
 
     def forward(j):
-        near_copy(j).wait_recv()
-
-        @pl.when(j < relayed)
-        def _():
-            relay_copy(j).start()
+        for k in range(PARTS):
+            near_copy(j, k).wait_recv()
+
+            @pl.when(j < relayed)
+            def _(k=k):
+                relay_copy(j, k).start()
 
     def finish(j):
         @pl.when(j < relayed)
         def _():
-            relay_copy(j).wait_recv()
+            for k in range(PARTS):
+                relay_copy(j, k).wait_recv()
 
         @pl.when(j >= relayed)
         def _():
@@ -416,7 +430,16 @@
                 guarded(finish, r - first - GOSSIP, chunks)
         return carry
 
-    lax.fori_loop(0, (chunks + first + GOSSIP + 1) // 2, body, 0)
+    turns = (chunks + first + 1) // 2
+    lax.fori_loop(0, turns, body, 0)
+
+    with jax.named_scope("tail"):
+        for t in range(2 * turns - first, chunks + max(RELAY, GOSSIP)):
+            if 0 <= t - GOSSIP < chunks:
+                finish(t - GOSSIP)
+            if 0 <= t - RELAY < chunks:
+                forward(t - RELAY)
+
 
     with jax.named_scope("drain"):
         to_sibling((), half_r.at[0, 0]).wait_send()
@@ -433,11 +456,13 @@
 
         @pl.when(edge == 0)
         def _():
-            for s in range(steps):
+            for s in range(1 if late else 0, steps):
                 sent(s, chunks - 1)
-
-        to_group(own, near, near_to, near_s, near_r.at[0], ()).wait_send()
-        to_group(own, far, far_to, far_s, far_r.at[0], ()).wait_send()
+            if late:
+                sent(2, chunks - 2)
+
+        to_group(own, near, near_to, near_s, near_r.at[0, 0], ()).wait_send()
+        to_group(own, far, far_to, far_s, far_r.at[0, 0], ()).wait_send()
 
 
 def flush(pieces, *refs):
@@ -491,7 +516,7 @@
             dma((7,)), dma((chunks.bit_length(),)), dma((3,)),
             dma, dma((3, 2)), dma((chips // 2, SLOTS)),
             dma((2, chips - 1, 2)), dma((2, chips - 1, ring)),
-            dma, dma((span,)), dma, dma((span + DIRECT,)),
+            dma, dma((span, PARTS)), dma, dma((span + DIRECT, PARTS)),
         ],
         compiler_params=pltpu.CompilerParams(
             collective_id=0, has_side_effects=True, vmem_limit_bytes=53 * 1024 * 1024

time: 85.1 us -> 84.5 us (level)
  no operation moved by 1% of the time
where the time goes in v3:
time: 84.5 us; the launch traced here: 84.3 us
  Pallas kernels  83.7 us (99%)
    pallas_call x1, Pallas kernels, on_device(): pl.pallas_call(functools.partial(kernel, cfg), out_shape=[pltpu.VMEM(para...  80.9 us
    pallas_call x1, Pallas kernels, on_device(): pl.pallas_call(functools.partial(flush, pieces), out_shape=[jax.ShapeDtyp...  2.75 us

profile of v3, /device:TPU:16, one launch (start us, length us, event | category | flops | bytes accessed | tf_op | source)
XLA Modules:
  0.0 84.3 jit_solution(7860964265867570181)
XLA Ops:
  0.6 80.9 %shard_map.94 = (f32[1,256,2048]{2,1,0:T(8,128)S(1)}, f32[1,256,2048]{2,1,0:T(8,128)S(1)}, f32[1,256,2048]{2,1,0:T(8,128)S(1)}) custom-call(f32[1,256,2048]{2,1,0:T(8,128)} %params.1, f32[1,256,2048]{2,1,0:T(8,128)} %estimate.1, f32[1,256,2048]{2,1,0:T(8,128)} %mixed.1, bf16[1024,2048]{1,0:T(8,128)(2,1)} %acts.1, bf16[1024,2048]{1,0:T(8,128)(2,1)} %grads.1, ...), custom_call_target="tpu_custom_call" | custom-call | tf_op jit(solution)/shard_map/pallas_call | solution.py:502
  81.6 2.8 %shard_map.95 = (f32[1,256,2048]{2,1,0:T(8,128)}, f32[1,256,2048]{2,1,0:T(8,128)}, f32[1,256,2048]{2,1,0:T(8,128)}) custom-call(f32[1,256,2048]{2,1,0:T(8,128)S(1)} %get-tuple-element.6.refs_0_, f32[1,256,2048]{2,1,0:T(8,128)S(1)} %get-tuple-element.7.refs_1_, f32[1,256,2048]{2,1,0:T(8,128)S(1)} %get-tuple-element.8.refs_2_), custom_call_target="tpu_custom_call" | custom-call | tf_op jit(solution)/shard_map/pallas_call | solution.py:526

commit v4 on v3

--- a/solution.py
+++ b/solution.py
@@ -18,7 +18,7 @@
 PIECES = 4
 SLOTS = 2
 STEP = 1
-RING = 6
+RING = 5
 PARTS = 2
 MESH = pl.DeviceIdType.MESH
 f32 = jnp.float32
@@ -32,7 +32,7 @@
     act_v, act_t, grad_v, par_v, est_v, mix_v,
     mine, give, got, line_out, line_in, own, near, far,
     act_sem, grad_sem, load_sem,
-    pair_s, half_r, pair_r, line_s, line_r, near_s, near_r, far_s, far_r,
+    pair_s, half_r, first_r, pair_r, line_s, line_r, near_s, near_r, far_s, far_r,
 ):
     members, groups, chunks, rows, width, tokens, factor = cfg
     chips = members // 2
@@ -48,7 +48,7 @@
     edge = jnp.where(chip < pairs, chip, chips - 1 - chip)
     inward = lax.rem(chip + chips + 1 - 2 * upper, chips) * 2 + core
     outward = lax.rem(chip + chips - 1 + 2 * upper, chips) * 2 + core
-    ways = ((upper, edge, inward), (1 - upper, chips - 1 - edge, outward))
+    ways = ((upper, edge, inward, 0), (1 - upper, chips - 1 - edge, outward, 1))
     odd = g % 2
     near_to = lax.rem(g + groups + 1 - 2 * odd, groups)
     far_to = lax.rem(g + groups - 1 + 2 * odd, groups)
@@ -94,15 +94,23 @@
     def half_copy(h, which):
         return to_sibling((half_at[h], which), half_r.at[h, which])
 
+    def first_copy(half):
+        return to_sibling((0, lead_which, half), half_r.at[0, lead_which] if half == 0 else first_r)
+
     def pair_copy(b, j):
         return to_sibling((b * (chunks // 2) + j,), pair_r.at[b, j % SLOTS])
 
     ring = line_r.shape[2]
+
+    def line_slot(way, s, j):
+        if way[3]:
+            return 2 * steps + jnp.minimum(s, pairs - 2)
+        return 2 * s + jnp.where(way[1] == 0, j % 2, 0)
 
     def line_copy(way, s, j):
         return pltpu.make_async_remote_copy(
             src_ref=line_out.at[way[0], s * chunks + j], dst_ref=line_in.at[way[0], s * chunks + j],
-            send_sem=line_s.at[way[0], s, jnp.where(way[1] == 0, j % 2, 0)], recv_sem=line_r.at[way[0], s, j % ring],
+            send_sem=line_s.at[line_slot(way, s, j)], recv_sem=line_r.at[way[0], s, j % ring],
             device_id={"mem": way[2]}, device_id_type=MESH,
         )
 
@@ -339,13 +347,19 @@
         put(give, 0, lead_which, product(lead, other, 0))
     with jax.named_scope("barrier"):
         pl.semaphore_wait(barrier, greeted)
-        half_copy(0, lead_which).start()
+        for half in (0, 1):
+            first_copy(half).start()
     with jax.named_scope("lead2"):
         load_block(lead * 2 + core, 1).wait()
         turn(lead * 2 + core)
         keep_half(lead, lead_which, 0)
-        half_copy(0, lead_which).wait_recv()
-        head(0, 0)
+        for half in (0, 1):
+            first_copy(half).wait_recv()
+
+            @pl.when(edge == 0)
+            def _(half=half):
+                pass_on(ways[0], 0, jnp.int32(half))
+
     with jax.named_scope("lead3"):
         grad_copy(1).wait()
         give_half(lead, lead_which, 1)
@@ -449,7 +463,7 @@
                 def _(way=way, s=s):
                     whole = line_out.at[way[0], pl.ds(s * chunks, chunks)]
                     pltpu.make_async_remote_copy(
-                        src_ref=whole, dst_ref=whole, send_sem=line_s.at[way[0], s, 0],
+                        src_ref=whole, dst_ref=whole, send_sem=line_s.at[line_slot(way, s, 0)],
                         recv_sem=line_r.at[way[0], s, 0],
                         device_id={"mem": way[2]}, device_id_type=MESH,
                     ).wait_send()
@@ -513,9 +527,9 @@
             pltpu.VMEM((2, slots, rows, cols), bf16),
             pltpu.VMEM((2, slots + chunks, rows, cols), bf16),
             *[pltpu.VMEM(wide, bf16)] * 3,
-            dma((7,)), dma((chunks.bit_length(),)), dma((3,)),
-            dma, dma((3, 2)), dma((chips // 2, SLOTS)),
-            dma((2, chips - 1, 2)), dma((2, chips - 1, ring)),
+            dma((7 if members > 8 else 6,)), dma((chunks.bit_length() - 1,)), dma((3,)),
+            dma, dma((3, 2)), dma, dma((chips // 2, SLOTS)),
+            dma((2 * (chips - 1) + chips // 2 - 1,)), dma((2, chips - 1, ring)),
             dma, dma((span, PARTS)), dma, dma((span + DIRECT, PARTS)),
         ],
         compiler_params=pltpu.CompilerParams(

time: 84.5 us -> 84.3 us (level)
  no operation moved by 1% of the time
where the time goes in v4:
time: 84.3 us; the launch traced here: 84.1 us
  Pallas kernels  83.5 us (99%)
    pallas_call x1, Pallas kernels, on_device(): pl.pallas_call(functools.partial(kernel, cfg), out_shape=[pltpu.VMEM(para...  80.8 us
    pallas_call x1, Pallas kernels, on_device(): pl.pallas_call(functools.partial(flush, pieces), out_shape=[jax.ShapeDtyp...  2.75 us

profile of v4, /device:TPU:16, one launch (start us, length us, event | category | flops | bytes accessed | tf_op | source)
XLA Modules:
  0.0 84.1 jit_solution(7335211724949940742)
XLA Ops:
  0.6 80.8 %shard_map.94 = (f32[1,256,2048]{2,1,0:T(8,128)S(1)}, f32[1,256,2048]{2,1,0:T(8,128)S(1)}, f32[1,256,2048]{2,1,0:T(8,128)S(1)}) custom-call(f32[1,256,2048]{2,1,0:T(8,128)} %params.1, f32[1,256,2048]{2,1,0:T(8,128)} %estimate.1, f32[1,256,2048]{2,1,0:T(8,128)} %mixed.1, bf16[1024,2048]{1,0:T(8,128)(2,1)} %acts.1, bf16[1024,2048]{1,0:T(8,128)(2,1)} %grads.1, ...), custom_call_target="tpu_custom_call" | custom-call | tf_op jit(solution)/shard_map/pallas_call | solution.py:516
  81.4 2.8 %shard_map.95 = (f32[1,256,2048]{2,1,0:T(8,128)}, f32[1,256,2048]{2,1,0:T(8,128)}, f32[1,256,2048]{2,1,0:T(8,128)}) custom-call(f32[1,256,2048]{2,1,0:T(8,128)S(1)} %get-tuple-element.6.refs_0_, f32[1,256,2048]{2,1,0:T(8,128)S(1)} %get-tuple-element.7.refs_1_, f32[1,256,2048]{2,1,0:T(8,128)S(1)} %get-tuple-element.8.refs_2_), custom_call_target="tpu_custom_call" | custom-call | tf_op jit(solution)/shard_map/pallas_call | solution.py:540

commit v5 on v4

--- a/solution.py
+++ b/solution.py
@@ -15,7 +15,7 @@
 RELAY = 1
 GOSSIP = 2
 DIRECT = 1
-PIECES = 4
+PIECES = 1
 SLOTS = 2
 STEP = 1
 RING = 5

time: 84.3 us -> 84.3 us (level)
  no operation moved by 1% of the time
where the time goes in v5:
time: 84.3 us; the launch traced here: 84.1 us
  Pallas kernels  83.5 us (99%)
    pallas_call x1, Pallas kernels, on_device(): pl.pallas_call(functools.partial(kernel, cfg), out_shape=[pltpu.VMEM(para...  80.8 us
    pallas_call x1, Pallas kernels, on_device(): pl.pallas_call(functools.partial(flush, pieces), out_shape=[jax.ShapeDtyp...  2.73 us

profile of v5, /device:TPU:16, one launch (start us, length us, event | category | flops | bytes accessed | tf_op | source)
XLA Modules:
  0.0 84.1 jit_solution(12545200277354155809)
XLA Ops:
  0.6 80.8 %shard_map.94 = (f32[1,256,2048]{2,1,0:T(8,128)S(1)}, f32[1,256,2048]{2,1,0:T(8,128)S(1)}, f32[1,256,2048]{2,1,0:T(8,128)S(1)}) custom-call(f32[1,256,2048]{2,1,0:T(8,128)} %params.1, f32[1,256,2048]{2,1,0:T(8,128)} %estimate.1, f32[1,256,2048]{2,1,0:T(8,128)} %mixed.1, bf16[1024,2048]{1,0:T(8,128)(2,1)} %acts.1, bf16[1024,2048]{1,0:T(8,128)(2,1)} %grads.1, ...), custom_call_target="tpu_custom_call" | custom-call | tf_op jit(solution)/shard_map/pallas_call | solution.py:516
  81.4 2.7 %shard_map.95 = (f32[1,256,2048]{2,1,0:T(8,128)}, f32[1,256,2048]{2,1,0:T(8,128)}, f32[1,256,2048]{2,1,0:T(8,128)}) custom-call(f32[1,256,2048]{2,1,0:T(8,128)S(1)} %get-tuple-element.6.refs_0_, f32[1,256,2048]{2,1,0:T(8,128)S(1)} %get-tuple-element.7.refs_1_, f32[1,256,2048]{2,1,0:T(8,128)S(1)} %get-tuple-element.8.refs_2_), custom_call_target="tpu_custom_call" | custom-call | tf_op jit(solution)/shard_map/pallas_call | solution.py:540
